TPU v7x, 32 devices: a whole 2x2x4 slice. The times are simulated.
32 devices in a mesh: section: 4 (over y, x), seq: 8 (over z, core).
Axes of the slice: x: 2, y: 2, z: 4, core: 2. Of those that a mesh axis runs over, the one named last changes fastest.
Arguments:
- stream: bfloat16 [4, 128, 1536], P('section', 'seq'), may hold values from -6 to 6
- queries: bfloat16 [4, 128, 1536], P('section', 'seq'), may hold values from -40 to 40
- fresh_keys: bfloat16 [4, 128, 1536], P('section', 'seq'), may hold values from -4 to 4
- fresh_values: bfloat16 [4, 128, 1536], P('section', 'seq'), may hold values from -6 to 6
- stale_keys: bfloat16 [4, 1536, 1536], P('section', 'seq'), may hold values from -6 to 6
- stale_values: bfloat16 [4, 1536, 1536], P('section', 'seq'), may hold values from -6 to 6
- gate: float32 [4, 1536], P('section'), may hold values from 0.5 to 4
- patch_of_section: int32 [4], P('section'), may hold values from 0 to 7, as said below
- text_len: int32 [1], replicated, may hold values from 128 to 512
Outputs:
- attended: bfloat16 [4, 128, 1536], P('section', 'seq')
- stream_next: bfloat16 [4, 128, 1536], P('section', 'seq')
Inputs may be any that keep to these rules, and one draw needn't show every extreme that they name: `patch_of_section`: section s works on patch (c - s) mod 8 for one c of the draw. The first text_len text positions are used.
All inputs are finite; a program needn't handle non-finite values.
Results may differ from a plain program's by a relative error of at most 0.0085.
Values may be sent and summed in bfloat16 or wider, within the bound.
A program may use at most 64 MiB of HBM per device.

v0:
```python
import math
import jax
import jax.numpy as jnp
from jax import lax
from jax.sharding import PartitionSpec as P

HEADS = 12
HDIM = 128
TXT = 512
FLOOR_SCORE = -1e30


def passed_along(value, axis, steps):
    count = lax.axis_size(axis)
    pairs = [(source, (source + steps) % count) for source in range(count)]
    return lax.ppermute(value, axis, pairs)


def head_scores(query_rows, key_rows):
    query_heads = query_rows.reshape(query_rows.shape[0], HEADS, HDIM)
    key_heads = key_rows.reshape(key_rows.shape[0], HEADS, HDIM)
    return jnp.einsum(
        "qhd,khd->hqk", query_heads, key_heads, preferred_element_type=jnp.float32
    ) / math.sqrt(HDIM)


def weighted_values(weights, value_rows):
    value_heads = value_rows.reshape(value_rows.shape[0], HEADS, HDIM)
    return jnp.einsum(
        "hqk,khd->qhd",
        weights.astype(jnp.bfloat16),
        value_heads,
        preferred_element_type=jnp.float32,
    )


def stale_allowed(first_row, piece_rows, patch_index, text_count, patch_length):
    positions = first_row + jnp.arange(piece_rows, dtype=jnp.int32)
    region = (positions - TXT) // patch_length
    return jnp.where(positions < TXT, positions < text_count, region != patch_index)


def local(
    stream,
    queries,
    fresh_keys,
    fresh_values,
    stale_keys,
    stale_values,
    gate,
    patch_of_section,
    text_len,
):
    incoming = passed_along(stream, "section", 1)
    row_count = queries.shape[1]
    patch_length = row_count * lax.axis_size("seq")
    patch_index = patch_of_section[0]
    text_count = text_len[0]
    everyone = lax.all_gather(queries, "seq", axis=1, tiled=True)[0]
    stale_rows = stale_keys.shape[1]
    key_rows = jnp.concatenate([stale_keys[0], fresh_keys[0]], 0)
    value_rows = jnp.concatenate([stale_values[0], fresh_values[0]], 0)
    first_row = lax.axis_index("seq") * stale_rows
    allowed = jnp.concatenate(
        [
            stale_allowed(first_row, stale_rows, patch_index, text_count, patch_length),
            jnp.ones((row_count,), dtype=bool),
        ],
        0,
    )
    scores = jnp.where(allowed[None, None, :], head_scores(everyone, key_rows), FLOOR_SCORE)
    local_max = jnp.max(scores, axis=2)
    global_max = lax.pmax(local_max, "seq")
    weights = jnp.where(allowed[None, None, :], jnp.exp(scores - local_max[:, :, None]), 0.0)
    factor = jnp.exp(local_max - global_max)
    partial_value = weighted_values(weights, value_rows) * jnp.transpose(factor)[:, :, None]
    partial_value = partial_value.reshape(patch_length, HEADS * HDIM)
    weight_sums = jnp.transpose(jnp.sum(weights, axis=2) * factor)
    weighted, row_sums = (
        lax.psum_scatter(partial_value, "seq", scatter_dimension=0, tiled=True),
        lax.psum_scatter(weight_sums, "seq", scatter_dimension=0, tiled=True),
    )
    averaged = weighted.reshape(row_count, HEADS, HDIM) / row_sums[:, :, None]
    attended = averaged.reshape(1, row_count, HEADS * HDIM).astype(jnp.bfloat16)
    stream_next = (
        incoming.astype(jnp.float32) + gate[:, None, :] * attended.astype(jnp.float32)
    ).astype(jnp.bfloat16)
    return (attended, stream_next)


def solution(mesh):
    placed = (
        P("section", "seq", None),
        P("section", "seq", None),
        P("section", "seq", None),
        P("section", "seq", None),
        P("section", "seq", None),
        P("section", "seq", None),
        P("section", None),
        P("section"),
        P(),
    )
    return jax.shard_map(
        local,
        mesh=mesh,
        in_specs=placed,
        out_specs=(P("section", "seq", None), P("section", "seq", None)),
        check_vma=False,
    )
```

profile of v0, /device:TPU:0, one launch (start us, length us, event | category | flops | bytes accessed | tf_op | source)
XLA Modules:
  0.0 116.1 jit_solution(6922269851643474781)
XLA Ops:
  7.2 0.0 reduce-scatter.7.cloned.1.call-start
  8.5 1.5 %concatenate.23 = bf16[192,12,128]{2,1,0:T(8,128)(2,1)S(1)} reshape(bf16[1,192,1536]{2,1,0:T(8,128)(2,1)} %param.13) | data formatting | bytes 1179648 | tf_op jit(solution)/shard_map/concatenate | solution.py:61
  10.0 0.2 copy.23
  10.2 16.2 %all_gather.3 = bf16[1,128,1536]{2,1,0:T(8,128)(2,1)S(1)} all-gather(bf16[1,16,1536]{2,1,0:T(8,128)(2,1)S(1)} %copy-done.1), channel_id=1, replica_groups=mesh['section'=4,'seq'=8] {'seq'}, dimensions={1}, use_global_device_ids=true | all-gather | bytes 442368 | tf_op jit(solution)/shard_map/all_gather | solution.py:59
  26.4 0.2 copy.25
  26.7 0.1 concatenate.24
  26.8 0.5 fusion.22
  27.3 17.3 %pmax.7 = f32[12,128]{1,0:T(8,128)S(1)} all-reduce(f32[12,128]{1,0:T(8,128)S(1)} %get-tuple-element.6), channel_id=1, replica_groups=mesh['section'=4,'seq'=8] {'seq'}, use_global_device_ids=true, to_apply=%region_1.2 | all-reduce | flops 1536 | bytes 12288 | tf_op jit(solution)/shard_map/pmax | solution.py:73
  44.6 0.2 fusion.3
  44.9 0.7 copy.30
  45.6 0.0 reduce-scatter.7.cloned.1.call-update
  45.7 0.0 reduce-scatter.5.cloned.1.call-start
  45.7 0.4 concatenate.19
  46.2 0.2 copy.21
  46.3 0.2 copy-done.3
  46.5 0.1 concatenate.20
  46.6 0.5 fusion.2
  47.1 1.1 copy.27
  48.2 0.0 reduce-scatter.5.cloned.1.call-update
  48.3 1.5 %collective-permute-start = (bf16[1,16,1536]{2,1,0:T(8,128)(2,1)S(1)}, bf16[1,16,1536]{2,1,0:T(8,128)(2,1)S(1)}, u32[]{:S(2)}, u32[]{:S(2)}) collective-permute-start(bf16[1,16,1536]{2,1,0:T(8,128)(2,1)S(1)} %copy-done.5), channel_id=1, source_target_pairs={{0,8},{8,16},{16,24},{24,0},{1,9},{9,17},{17,25},{25,1},{2,10},{10... | collective-permute-start | bytes 147464 | tf_op jit(solution)/shard_map/ppermute | solution.py:16
  49.8 24.8 %reduce-scatter.7.cloned.1.call-done = f32[16,12]{1,0:T(8,128)} async-done(((f32[128,12]{1,0:T(8,128)}), f32[16,12]{1,0:T(8,128)}) %reduce-scatter.7.cloned.1.call-update) | async-done | bytes 784 | tf_op jit(solution)/shard_map/reduce_scatter | solution.py:81
  74.6 32.3 %reduce-scatter.5.cloned.1.call-done = f32[16,1536]{1,0:T(8,128)} async-done(((f32[128,1536]{1,0:T(8,128)}), f32[16,1536]{1,0:T(8,128)}) %reduce-scatter.5.cloned.1.call-update) | async-done | bytes 98320 | tf_op jit(solution)/shard_map/reduce_scatter | solution.py:80
  106.9 0.8 div.35
  107.7 1.6 %fusion.16 = (bf16[1,16,1536]{2,1,0:T(8,128)(2,1)}, bf16[16,1536]{1,0:T(8,128)(2,1)}) fusion(bf16[1,16,1536]{2,1,0:T(8,128)(2,1)S(1)} %collective-permute-done, f32[1536]{0:T(1024)S(1)} %reduce, f32[16,1536]{1,0:T(8,128)} %reduce-scatter.5.cloned.1.call-done, f32[2,8,12,128]{3,2,1,0:T(8,128)S(1)} %bitcast.30), kind=kLoop, calls=%fused_computation.20 | loop fusion | flops 172032 | bytes 350208 | tf_op jit(solution)/shard_map/convert_element_type | solution.py:87
  (18 shorter events, 0.1 us)
Async XLA Ops:
  7.2 67.4 %reduce-scatter.7.cloned.1.call-start = ((), (), s32[]{:S(2)}) async-start(), calls=%async_computation.3 | async-start | bytes 73728 | tf_op jit(solution)/shard_map/reduce_scatter | solution.py:81
  8.5 1.7 %copy-start.1 = (bf16[1,16,1536]{2,1,0:T(8,128)(2,1)S(1)}, bf16[1,16,1536]{2,1,0:T(8,128)(2,1)}, u32[]{:S(2)}) copy-start(bf16[1,16,1536]{2,1,0:T(8,128)(2,1)} %param.10) | copy-start | bytes 147460
  10.0 16.6 %copy-start.2 = (bf16[1,16,1536]{2,1,0:T(8,128)(2,1)S(1)}, bf16[1,16,1536]{2,1,0:T(8,128)(2,1)}, u32[]{:S(2)}) copy-start(bf16[1,16,1536]{2,1,0:T(8,128)(2,1)} %param.11) | copy-start | bytes 147460
  27.3 18.4 %copy-start = (bf16[1,192,1536]{2,1,0:T(8,128)(2,1)S(1)}, bf16[1,192,1536]{2,1,0:T(8,128)(2,1)}, u32[]{:S(2)}) copy-start(bf16[1,192,1536]{2,1,0:T(8,128)(2,1)} %param.14) | copy-start | bytes 1769476
  45.7 0.8 copy-start.3
  45.7 61.2 %reduce-scatter.5.cloned.1.call-start = ((), (), s32[]{:S(2)}) async-start(), calls=%async_computation.2 | async-start | bytes 884736 | tf_op jit(solution)/shard_map/reduce_scatter | solution.py:80
  47.0 1.2 %copy-start.5 = (bf16[1,16,1536]{2,1,0:T(8,128)(2,1)S(1)}, bf16[1,16,1536]{2,1,0:T(8,128)(2,1)}, u32[]{:S(2)}) copy-start(bf16[1,16,1536]{2,1,0:T(8,128)(2,1)} %param.9) | copy-start | bytes 147460
  47.1 2.7 %copy-start.4 = (f32[1,1536]{1,0:T(1,128)S(1)}, f32[1,1536]{1,0:T(1,128)}, u32[]{:S(2)}) copy-start(f32[1,1536]{1,0:T(1,128)} %param.15) | copy-start | bytes 18436
  48.3 26.3 %collective-permute-start = (bf16[1,16,1536]{2,1,0:T(8,128)(2,1)S(1)}, bf16[1,16,1536]{2,1,0:T(8,128)(2,1)S(1)}, u32[]{:S(2)}, u32[]{:S(2)}) collective-permute-start(bf16[1,16,1536]{2,1,0:T(8,128)(2,1)S(1)} %copy-done.5), channel_id=1, source_target_pairs={{0,8},{8,16},{16,24},{24,0},{1,9},{9,17},{17,25},{25,1},{2,10},{10... | collective-permute-start | bytes 147464 | tf_op jit(solution)/shard_map/ppermute | solution.py:16
Sparse Core Ops, SparseCore 0:
  45.8 28.7 reduce-scatter.6
  76.9 30.0 reduce-scatter.4
where the time goes:
time: 116 us
  waiting for transfers between devices  57.1 us (49%)
  blocking collectives  33.6 us (29%)
  between operations  15.5 us (13%)
  local copies, waits for them, and re-layouts  5.43 us (5%)
  other arithmetic  1.87 us (2%)
  starting transfers between devices  1.63 us (1%)
    reduce_scatter x1, waiting for transfers between devices, local(): lax.psum_scatter(partial_value, 'seq', scatter_dimension=0, tiled=True)  32.3 us
    reduce_scatter x1, waiting for transfers between devices, local(): lax.psum_scatter(weight_sums, 'seq', scatter_dimension=0, tiled=True)  24.8 us
    pmax x1, blocking collectives, local(): global_max = lax.pmax(local_max, 'seq')  17.3 us
    all_gather x1, blocking collectives, local(): everyone = lax.all_gather(queries, 'seq', axis=1, tiled=True)[0]  16.2 us
  transfers between devices with their start and end apart: 3, of which 2 were waited for; matrix products, arithmetic and copies ran while one was open for 2% of the time, Pallas kernels for 0%

commit v1 on v0

--- a/solution.py
+++ b/solution.py
@@ -8,6 +8,34 @@
 HDIM = 128
 TXT = 512
 FLOOR_SCORE = -1e30
+
+
+def follow_the_panel(vec, d_out):
+    vec = jnp.moveaxis(vec, 0, d_out)
+    clean = vec.shape
+    return vec.reshape(*clean[:d_out], clean[d_out] * clean[d_out + 1], *clean[d_out + 2 :])
+
+
+def refer_the_members_all(array_here, axis_tag, dim_i=1):
+    nodes = lax.axis_size(axis_tag)
+    so_far_all = [(p, (p + 1) % nodes) for p in range(nodes)]
+    fields = [(tick, dev_j) for dev_j, tick in so_far_all]
+    w1, step_out = ([], [])
+    no = 0
+    while no < nodes - 1:
+        if no % 2 == 0:
+            carry_out = lax.ppermute(w1[-1] if w1 else array_here, axis_tag, so_far_all)
+            w1.append(carry_out)
+        else:
+            finding = lax.ppermute(step_out[-1] if step_out else array_here, axis_tag, fields)
+            step_out.append(finding)
+        no += 1
+    b_next = jnp.stack([*w1[::-1], array_here, *step_out], axis=0)
+    z = lax.axis_index(axis_tag)
+    out_arr = len(w1)
+    e_now = z - out_arr
+    b_next = b_next[(jnp.arange(nodes) - e_now) % nodes]
+    return follow_the_panel(b_next, dim_i)
 
 
 def passed_along(value, axis, steps):
@@ -56,7 +84,7 @@
     patch_length = row_count * lax.axis_size("seq")
     patch_index = patch_of_section[0]
     text_count = text_len[0]
-    everyone = lax.all_gather(queries, "seq", axis=1, tiled=True)[0]
+    everyone = refer_the_members_all(queries, "seq")[0]
     stale_rows = stale_keys.shape[1]
     key_rows = jnp.concatenate([stale_keys[0], fresh_keys[0]], 0)
     value_rows = jnp.concatenate([stale_values[0], fresh_values[0]], 0)

time: 116 us -> 124 us (1.069)
  blocking collectives: 33.6 us -> 17.4 us
  starting transfers between devices: 1.63 us -> 14.2 us
  waiting for transfers between devices: 57.1 us -> 67.4 us
    all_gather x1 -> x0, blocking collectives: 16.2 us -> none  [local(): everyone = lax.all_gather(queries, 'seq', axis=1, tiled=True)[0]]
    ppermute x0 -> x7, starting transfers between devices: none -> 11.8 us  [the longest x3 11.3 us: refer_the_members_all(): lax.ppermute(step_out[-1] if step_out else array_here, axis_tag, fields)]
    ppermute x0 -> x7, waiting for transfers between devices: none -> 9.44 us  [the longest x4 7.78 us: refer_the_members_all(): carry_out = lax.ppermute(w1[-1] if w1 else array_here, axis_tag, so_far_all)]
    ppermute x1, waiting for transfers between devices: 0.01 us -> 2.99 us  [passed_along(): return lax.ppermute(value, axis, pairs)]
    reduce_scatter x1, waiting for transfers between devices: 24.8 us -> 22.6 us  [local(): lax.psum_scatter(weight_sums, 'seq', scatter_dimension=0, tiled=True)]
  transfers between devices with their start and end apart: 3 -> 10, of which waited for: 2 -> 7; matrix products, arithmetic and copies ran while one was open for 2% -> 3% of each run, Pallas kernels for 0% -> 0%
where the time goes in v1:
time: 124 us
  waiting for transfers between devices  67.4 us (54%)
  blocking collectives  17.4 us (14%)
  between operations  15.6 us (13%)
  starting transfers between devices  14.2 us (11%)
  local copies, waits for them, and re-layouts  6.24 us (5%)
  other arithmetic  1.89 us (2%)
    reduce_scatter x1, waiting for transfers between devices, local(): lax.psum_scatter(partial_value, 'seq', scatter_dimension=0, tiled=True)  32.3 us
    reduce_scatter x1, waiting for transfers between devices, local(): lax.psum_scatter(weight_sums, 'seq', scatter_dimension=0, tiled=True)  22.6 us
    pmax x1, blocking collectives, local(): global_max = lax.pmax(local_max, 'seq')  17.4 us
    ppermute x3, starting transfers between devices, refer_the_members_all(): lax.ppermute(step_out[-1] if step_out else array_here, axis_tag, fields)  11.3 us
    ppermute x4, waiting for transfers between devices, refer_the_members_all(): carry_out = lax.ppermute(w1[-1] if w1 else array_here, axis_tag, so_far_all)  7.78 us
    ppermute x1, waiting for transfers between devices, passed_along(): return lax.ppermute(value, axis, pairs)  2.99 us
  transfers between devices with their start and end apart: 10, of which 7 were waited for; matrix products, arithmetic and copies ran while one was open for 3% of the time, Pallas kernels for 0%

profile of v1, /device:TPU:0, one launch (start us, length us, event | category | flops | bytes accessed | tf_op | source)
XLA Modules:
  0.0 123.7 jit_solution(8661754062067174157)
XLA Ops:
  7.2 0.5 collective-permute-start
  7.8 4.1 %collective-permute-start.4 = (bf16[1,16,1536]{2,1,0:T(8,128)(2,1)}, bf16[1,16,1536]{2,1,0:T(8,128)(2,1)S(1)}, u32[]{:S(2)}, u32[]{:S(2)}) collective-permute-start(bf16[1,16,1536]{2,1,0:T(8,128)(2,1)} %param.10), channel_id=1, source_target_pairs={{1,0},{2,1},{3,2},{4,3},{5,4},{6,5},{7,6},{0,7},{9,8},{10,9},{11,1... | collective-permute-start | bytes 147464 | tf_op jit(solution)/shard_map/ppermute | solution.py:30
  11.8 1.9 %collective-permute-done = bf16[1,16,1536]{2,1,0:T(8,128)(2,1)S(1)} collective-permute-done((bf16[1,16,1536]{2,1,0:T(8,128)(2,1)}, bf16[1,16,1536]{2,1,0:T(8,128)(2,1)S(1)}, u32[]{:S(2)}, u32[]{:S(2)}) %collective-permute-start) | collective-permute-done | bytes 49184 | tf_op jit(solution)/shard_map/ppermute | solution.py:27
  13.8 5.3 %collective-permute-done.1 = bf16[1,16,1536]{2,1,0:T(8,128)(2,1)S(1)} collective-permute-done((bf16[1,16,1536]{2,1,0:T(8,128)(2,1)S(1)}, bf16[1,16,1536]{2,1,0:T(8,128)(2,1)S(1)}, u32[]{:S(2)}, u32[]{:S(2)}) %collective-permute-start.1) | collective-permute-done | bytes 49184 | tf_op jit(solution)/shard_map/ppermute | solution.py:27
  20.4 3.6 %collective-permute-start.5 = (bf16[1,16,1536]{2,1,0:T(8,128)(2,1)S(1)}, bf16[1,16,1536]{2,1,0:T(8,128)(2,1)S(1)}, u32[]{:S(2)}, u32[]{:S(2)}) collective-permute-start(bf16[1,16,1536]{2,1,0:T(8,128)(2,1)S(1)} %collective-permute-done.4), channel_id=1, source_target_pairs={{1,0},{2,1},{3,2},{4,3},{5,4},{6,5},{7,6},{0,7},{9,8},{10,9},{11,1... | collective-permute-start | bytes 147464 | tf_op jit(solution)/shard_map/ppermute | solution.py:30
  24.0 0.6 collective-permute-done.2
  24.6 1.6 %concatenate.23 = bf16[192,12,128]{2,1,0:T(8,128)(2,1)S(1)} reshape(bf16[1,192,1536]{2,1,0:T(8,128)(2,1)} %param.13) | data formatting | bytes 1179648 | tf_op jit(solution)/shard_map/concatenate | solution.py:89
  26.4 0.4 concatenate.19
  27.3 3.6 %collective-permute-start.6 = (bf16[1,16,1536]{2,1,0:T(8,128)(2,1)S(1)}, bf16[1,16,1536]{2,1,0:T(8,128)(2,1)S(1)}, u32[]{:S(2)}, u32[]{:S(2)}) collective-permute-start(bf16[1,16,1536]{2,1,0:T(8,128)(2,1)S(1)} %collective-permute-done.5), channel_id=1, source_target_pairs={{1,0},{2,1},{3,2},{4,3},{5,4},{6,5},{7,6},{0,7},{9,8},{10,9},{11,1... | collective-permute-start | bytes 147464 | tf_op jit(solution)/shard_map/ppermute | solution.py:30
  31.0 1.7 %collective-permute-done.6 = bf16[1,16,1536]{2,1,0:T(8,128)(2,1)S(1)} collective-permute-done((bf16[1,16,1536]{2,1,0:T(8,128)(2,1)S(1)}, bf16[1,16,1536]{2,1,0:T(8,128)(2,1)S(1)}, u32[]{:S(2)}, u32[]{:S(2)}) %collective-permute-start.6) | collective-permute-done | bytes 49184 | tf_op jit(solution)/shard_map/ppermute | solution.py:30
  32.7 0.6 gather_fusion
  33.3 0.3 reshape_squeeze_reshape_transpose.3
  33.5 0.5 fusion.24
  34.1 17.4 %pmax.7 = f32[12,128]{1,0:T(8,128)S(1)} all-reduce(f32[12,128]{1,0:T(8,128)S(1)} %get-tuple-element.6), channel_id=1, replica_groups=mesh['section'=4,'seq'=8] {'seq'}, use_global_device_ids=true, to_apply=%region_1.2 | all-reduce | flops 1536 | bytes 12288 | tf_op jit(solution)/shard_map/pmax | solution.py:101
  51.5 0.2 fusion.2
  51.7 0.7 copy.28
  52.6 0.5 fusion.1
  53.1 1.2 copy.26
  54.3 2.3 %collective-permute-start.7 = (bf16[1,16,1536]{2,1,0:T(8,128)(2,1)S(1)}, bf16[1,16,1536]{2,1,0:T(8,128)(2,1)S(1)}, u32[]{:S(2)}, u32[]{:S(2)}) collective-permute-start(bf16[1,16,1536]{2,1,0:T(8,128)(2,1)S(1)} %copy-done.5), channel_id=1, source_target_pairs={{0,8},{8,16},{16,24},{24,0},{1,9},{9,17},{17,25},{25,1},{2,10},{10... | collective-permute-start | bytes 147464 | tf_op jit(solution)/shard_map/ppermute | solution.py:44
  56.6 3.0 %collective-permute-done.7 = bf16[1,16,1536]{2,1,0:T(8,128)(2,1)S(1)} collective-permute-done((bf16[1,16,1536]{2,1,0:T(8,128)(2,1)S(1)}, bf16[1,16,1536]{2,1,0:T(8,128)(2,1)S(1)}, u32[]{:S(2)}, u32[]{:S(2)}) %collective-permute-start.7) | collective-permute-done | bytes 49184 | tf_op jit(solution)/shard_map/ppermute | solution.py:44
  59.6 22.6 %reduce-scatter.7.cloned.1.call-done = f32[16,12]{1,0:T(8,128)} async-done(((f32[128,12]{1,0:T(8,128)}), f32[16,12]{1,0:T(8,128)}) %reduce-scatter.7.cloned.1.call-update) | async-done | bytes 784 | tf_op jit(solution)/shard_map/reduce_scatter | solution.py:109
  82.2 32.3 %reduce-scatter.5.cloned.1.call-done = f32[16,1536]{1,0:T(8,128)} async-done(((f32[128,1536]{1,0:T(8,128)}), f32[16,1536]{1,0:T(8,128)}) %reduce-scatter.5.cloned.1.call-update) | async-done | bytes 98320 | tf_op jit(solution)/shard_map/reduce_scatter | solution.py:108
  114.5 0.8 div.35
  115.3 1.6 %fusion.16 = (bf16[1,16,1536]{2,1,0:T(8,128)(2,1)}, bf16[16,1536]{1,0:T(8,128)(2,1)}) fusion(bf16[1,16,1536]{2,1,0:T(8,128)(2,1)S(1)} %collective-permute-done.7, f32[1536]{0:T(1024)S(1)} %reduce, f32[16,1536]{1,0:T(8,128)} %reduce-scatter.5.cloned.1.call-done, f32[2,8,12,128]{3,2,1,0:T(8,128)S(1)} %bitcast.45), kind=kLoop, calls=%fused_computation.21 | loop fusion | flops 172032 | bytes 350208 | tf_op jit(solution)/shard_map/convert_element_type | solution.py:115
  (42 shorter events, 0.9 us)
Async XLA Ops:
  7.2 75.0 %reduce-scatter.7.cloned.1.call-start = ((), (), s32[]{:S(2)}) async-start(), calls=%async_computation.3 | async-start | bytes 73728 | tf_op jit(solution)/shard_map/reduce_scatter | solution.py:109
  7.2 6.6 %collective-permute-start = (bf16[1,16,1536]{2,1,0:T(8,128)(2,1)}, bf16[1,16,1536]{2,1,0:T(8,128)(2,1)S(1)}, u32[]{:S(2)}, u32[]{:S(2)}) collective-permute-start(bf16[1,16,1536]{2,1,0:T(8,128)(2,1)} %param.10), channel_id=1, source_target_pairs={{0,1},{1,2},{2,3},{3,4},{4,5},{5,6},{6,7},{7,0},{8,9},{9,10},{10,1... | collective-permute-start | bytes 147464 | tf_op jit(solution)/shard_map/ppermute | solution.py:27
  7.8 12.6 %collective-permute-start.4 = (bf16[1,16,1536]{2,1,0:T(8,128)(2,1)}, bf16[1,16,1536]{2,1,0:T(8,128)(2,1)S(1)}, u32[]{:S(2)}, u32[]{:S(2)}) collective-permute-start(bf16[1,16,1536]{2,1,0:T(8,128)(2,1)} %param.10), channel_id=1, source_target_pairs={{1,0},{2,1},{3,2},{4,3},{5,4},{6,5},{7,6},{0,7},{9,8},{10,9},{11,1... | collective-permute-start | bytes 147464 | tf_op jit(solution)/shard_map/ppermute | solution.py:30
  13.8 5.3 %collective-permute-start.1 = (bf16[1,16,1536]{2,1,0:T(8,128)(2,1)S(1)}, bf16[1,16,1536]{2,1,0:T(8,128)(2,1)S(1)}, u32[]{:S(2)}, u32[]{:S(2)}) collective-permute-start(bf16[1,16,1536]{2,1,0:T(8,128)(2,1)S(1)} %collective-permute-done), channel_id=1, source_target_pairs={{0,1},{1,2},{2,3},{3,4},{4,5},{5,6},{6,7},{7,0},{8,9},{9,10},{10,1... | collective-permute-start | bytes 147464 | tf_op jit(solution)/shard_map/ppermute | solution.py:27
  19.1 5.5 %collective-permute-start.2 = (bf16[1,16,1536]{2,1,0:T(8,128)(2,1)S(1)}, bf16[1,16,1536]{2,1,0:T(8,128)(2,1)S(1)}, u32[]{:S(2)}, u32[]{:S(2)}) collective-permute-start(bf16[1,16,1536]{2,1,0:T(8,128)(2,1)S(1)} %collective-permute-done.1), channel_id=1, source_target_pairs={{0,1},{1,2},{2,3},{3,4},{4,5},{5,6},{6,7},{7,0},{8,9},{9,10},{10,1... | collective-permute-start | bytes 147464 | tf_op jit(solution)/shard_map/ppermute | solution.py:27
  20.4 6.9 %collective-permute-start.5 = (bf16[1,16,1536]{2,1,0:T(8,128)(2,1)S(1)}, bf16[1,16,1536]{2,1,0:T(8,128)(2,1)S(1)}, u32[]{:S(2)}, u32[]{:S(2)}) collective-permute-start(bf16[1,16,1536]{2,1,0:T(8,128)(2,1)S(1)} %collective-permute-done.4), channel_id=1, source_target_pairs={{1,0},{2,1},{3,2},{4,3},{5,4},{6,5},{7,6},{0,7},{9,8},{10,9},{11,1... | collective-permute-start | bytes 147464 | tf_op jit(solution)/shard_map/ppermute | solution.py:30
  24.6 6.4 %collective-permute-start.3 = (bf16[1,16,1536]{2,1,0:T(8,128)(2,1)S(1)}, bf16[1,16,1536]{2,1,0:T(8,128)(2,1)S(1)}, u32[]{:S(2)}, u32[]{:S(2)}) collective-permute-start(bf16[1,16,1536]{2,1,0:T(8,128)(2,1)S(1)} %collective-permute-done.2), channel_id=1, source_target_pairs={{0,1},{1,2},{2,3},{3,4},{4,5},{5,6},{6,7},{7,0},{8,9},{9,10},{10,1... | collective-permute-start | bytes 147464 | tf_op jit(solution)/shard_map/ppermute | solution.py:27
  24.6 1.8 %copy-start.1 = (bf16[1,16,1536]{2,1,0:T(8,128)(2,1)S(1)}, bf16[1,16,1536]{2,1,0:T(8,128)(2,1)}, u32[]{:S(2)}) copy-start(bf16[1,16,1536]{2,1,0:T(8,128)(2,1)} %param.11) | copy-start | bytes 147460
  24.6 1.8 %copy-start = (bf16[1,192,1536]{2,1,0:T(8,128)(2,1)S(1)}, bf16[1,192,1536]{2,1,0:T(8,128)(2,1)}, u32[]{:S(2)}) copy-start(bf16[1,192,1536]{2,1,0:T(8,128)(2,1)} %param.14) | copy-start | bytes 1769476
  26.4 0.8 copy-start.2
  26.9 4.1 %copy-start.3 = (bf16[1,16,1536]{2,1,0:T(8,128)(2,1)S(1)}, bf16[1,16,1536]{2,1,0:T(8,128)(2,1)}, u32[]{:S(2)}) copy-start(bf16[1,16,1536]{2,1,0:T(8,128)(2,1)} %param.10) | copy-start | bytes 147460
  27.3 5.3 %collective-permute-start.6 = (bf16[1,16,1536]{2,1,0:T(8,128)(2,1)S(1)}, bf16[1,16,1536]{2,1,0:T(8,128)(2,1)S(1)}, u32[]{:S(2)}, u32[]{:S(2)}) collective-permute-start(bf16[1,16,1536]{2,1,0:T(8,128)(2,1)S(1)} %collective-permute-done.5), channel_id=1, source_target_pairs={{1,0},{2,1},{3,2},{4,3},{5,4},{6,5},{7,6},{0,7},{9,8},{10,9},{11,1... | collective-permute-start | bytes 147464 | tf_op jit(solution)/shard_map/ppermute | solution.py:30
  52.5 62.0 %reduce-scatter.5.cloned.1.call-start = ((), (), s32[]{:S(2)}) async-start(), calls=%async_computation.2 | async-start | bytes 884736 | tf_op jit(solution)/shard_map/reduce_scatter | solution.py:108
  53.1 1.2 copy-start.5
  53.1 3.5 %copy-start.4 = (f32[1,1536]{1,0:T(1,128)S(1)}, f32[1,1536]{1,0:T(1,128)}, u32[]{:S(2)}) copy-start(f32[1,1536]{1,0:T(1,128)} %param.15) | copy-start | bytes 18436
  54.3 5.3 %collective-permute-start.7 = (bf16[1,16,1536]{2,1,0:T(8,128)(2,1)S(1)}, bf16[1,16,1536]{2,1,0:T(8,128)(2,1)S(1)}, u32[]{:S(2)}, u32[]{:S(2)}) collective-permute-start(bf16[1,16,1536]{2,1,0:T(8,128)(2,1)S(1)} %copy-done.5), channel_id=1, source_target_pairs={{0,8},{8,16},{16,24},{24,0},{1,9},{9,17},{17,25},{25,1},{2,10},{10... | collective-permute-start | bytes 147464 | tf_op jit(solution)/shard_map/ppermute | solution.py:44
Sparse Core Ops, SparseCore 0:
  52.6 29.4 reduce-scatter.6
  84.4 30.0 reduce-scatter.4
